TPU v7x, 512 devices: a whole 4x8x8 slice. The times are simulated.
512 devices in a mesh: expert: 8 (over x, core), shard: 64 (over y, z).
Axes of the slice: x: 4, y: 8, z: 8, core: 2. Of those that a mesh axis runs over, the one named last changes fastest.
Arguments:
- tokens: bfloat16 [384, 4096], P('shard', 'expert'), may hold values from -6 to 6
- expert_ids: int32 [384, 2], P('shard'), may hold values from 0 to 7, all different within a row; in each aligned block of 6 rows (0 to 5, 6 to 11, ...) at most 3 rows name the same one
- gates: float32 [384, 2], P('shard'), may hold values from 0.1 to 1
- gate_proj: bfloat16 [8, 4096, 8192], P('expert', None, 'shard'), may hold values from -0.09375 to 0.09375
- up_proj: bfloat16 [8, 4096, 8192], P('expert', None, 'shard'), may hold values from -0.09375 to 0.09375
- down_proj_t: bfloat16 [8, 4096, 8192], P('expert', 'shard'), may hold values from -0.0625 to 0.0625
Outputs:
- mixed: bfloat16 [384, 4096], P('shard', 'expert')
Inputs may be any that keep to these rules, and one draw needn't show every extreme that they name: `expert_ids`: each token names two different experts; among the 6 tokens of one aligned block no expert is named more than 3 times, and in every draw some expert is named exactly 3 times in some block.
All inputs are finite; a program needn't handle non-finite values.
Results may differ from a plain program's by a relative error of at most 0.0085.
Values may be sent and summed in bfloat16 or wider, within the bound.
A program may use at most 64 MiB of HBM per device.

v0:
```python
import jax
import jax.numpy as jnp
from jax import lax
from jax.sharding import Mesh
from jax.sharding import PartitionSpec as P

SHARD = ("shard_0", "shard_1")


def in_order(parts, dim):
    parts = jnp.moveaxis(parts, 0, dim)
    lengths = parts.shape
    return parts.reshape(*lengths[:dim], lengths[dim] * lengths[dim + 1], *lengths[dim + 2 :])


def all_blocks(value, axes, turns):
    parts = value[None]
    for k in turns:
        parts = lax.all_gather(parts, axes[k], axis=0, tiled=True)
    held = [lax.axis_size(axes[k]) for k in reversed(turns)]
    parts = parts.reshape(*held, *value.shape)
    turned = sorted(range(len(turns)), key=lambda place: turns[len(turns) - 1 - place])
    return parts.transpose(*turned, *range(len(turns), parts.ndim)).reshape(-1, *value.shape)


def gathered_by_axis(value, axes, turns, dim):
    return in_order(all_blocks(value, axes, turns), dim)


def in_blocks(value, dim, length):
    before, after = (value.shape[:dim], value.shape[dim + 1 :])
    return jnp.moveaxis(value.reshape(*before, length, -1, *after), dim, 0)


def sum_at_owner(value, axis, dim):
    length = lax.axis_size(axis)
    parts = lax.all_to_all(in_blocks(value, dim, length), axis, 0, 0, tiled=True)
    return jnp.sum(parts.astype(jnp.float32), axis=0)


def shards(tokens, expert_ids, gates, gate_proj, up_proj, down_proj_t):
    experts = lax.axis_size("expert")
    tok_count = tokens.shape[0]
    capacity = min(tok_count, 4 * tok_count // experts)
    expert_range = jnp.arange(experts, dtype=jnp.int32)
    matches = expert_ids[:, :, None] == expert_range[None, None, :]
    routed = jnp.sum(matches.astype(jnp.int32), axis=1)
    weight = jnp.sum(gates[:, :, None] * matches.astype(jnp.float32), axis=1)
    slot_rank = jnp.cumsum(routed, axis=0) - routed
    slot_range = jnp.arange(capacity, dtype=jnp.int32)
    selector = (slot_rank.T[:, None, :] == slot_range[None, :, None]) & (routed.T[:, None, :] > 0)
    selector_bf = selector.astype(jnp.bfloat16)
    outgoing = jnp.einsum(
        "ect,td->ecd", selector_bf, tokens, preferred_element_type=jnp.float32
    ).astype(jnp.bfloat16)
    arrived = lax.all_to_all(outgoing, "expert", split_axis=0, concat_axis=2, tiled=True)
    own_rows = arrived[0]
    gate_local = gate_proj[0]
    up_local = up_proj[0]
    down_local = down_proj_t[0]
    piece = gathered_by_axis(own_rows, SHARD, (0, 1), 0)
    gate_out = jnp.dot(piece, gate_local, preferred_element_type=jnp.float32)
    up_out = jnp.dot(piece, up_local, preferred_element_type=jnp.float32)
    hidden = (jax.nn.silu(gate_out) * up_out).astype(jnp.bfloat16)
    down_rows = lax.all_to_all(down_local, SHARD, split_axis=1, concat_axis=0, tiled=True)
    expert_out = sum_at_owner(
        lax.dot_general(
            hidden, down_rows, (((1,), (1,)), ((), ())), preferred_element_type=jnp.float32
        ).astype(jnp.bfloat16),
        SHARD,
        0,
    ).astype(jnp.bfloat16)
    gathered_out = lax.all_to_all(expert_out, "expert", split_axis=1, concat_axis=0, tiled=True)
    combiner = (
        (selector.astype(jnp.float32) * weight.T[:, None, :])
        .reshape(experts * capacity, tok_count)
        .T
    )
    mixed_sum = jnp.dot(combiner, gathered_out.astype(jnp.float32), precision=lax.Precision.HIGHEST)
    return mixed_sum.astype(jnp.bfloat16)


def solution(mesh):
    split = Mesh(mesh.devices.reshape(mesh.shape["expert"], 8, 8), ("expert", "shard_0", "shard_1"))
    placed = (
        P(SHARD, "expert"),
        P(SHARD, None),
        P(SHARD, None),
        P("expert", None, SHARD),
        P("expert", None, SHARD),
        P("expert", SHARD, None),
    )
    return jax.shard_map(
        shards, mesh=split, in_specs=placed, out_specs=P(SHARD, "expert"), check_vma=False
    )
```

profile of v0, /device:TPU:24, one launch (start us, length us, event | category | flops | bytes accessed | tf_op | source)
XLA Modules:
  0.0 202.7 jit_solution(2765780398806376705)
XLA Ops:
  6.5 0.0 copy-start
  6.5 0.0 copy-start.1
  6.5 0.0 all-gather.2.cloned.1.call-start
  6.5 0.9 copy.27
  7.5 0.1 convert_reduce_fusion
  7.6 0.9 convolution_convert_fusion.1
  8.5 9.5 %all_to_all.58 = bf16[8,3,512]{2,1,0:T(4,128)(2,1)S(1)} all-to-all(bf16[8,3,512]{2,1,0:T(4,128)(2,1)S(1)} %copy.30), channel_id=1, replica_groups=mesh['expert'=8,'shard_0'=8,'shard_1'=8] {'expert'}, dimensions={0} | all-to-all | bytes 49152 | tf_op jit(solution)/shard_map/all_to_all | solution.py:56
  18.0 25.0 %all_gather.6 = bf16[8,3,4096]{2,1,0:T(4,128)(2,1)S(1)} all-gather(bf16[1,3,4096]{2,1,0:T(4,128)(2,1)S(1)} %bitcast.43), channel_id=1, replica_groups=mesh['expert'=8,'shard_0'=8,'shard_1'=8] {'shard_0'}, dimensions={0}, use_global_device_ids=true | all-gather | bytes 221184 | tf_op jit(solution)/shard_map/all_gather | solution.py:19
  43.1 0.8 copy.31
  43.9 0.0 all-gather.2.cloned.1.call-update
  43.9 0.0 copy-done.1
  43.9 0.3 copy.36
  44.2 1.7 copy.33
  45.9 16.5 %all-to-all-start.1 = ((bf16[64,64,128]{2,0,1:T(8,128)(2,1)}), bf16[64,64,128]{2,0,1:T(8,128)(2,1)}, u32[]{:S(2)}, u32[]{:S(2)}) async-start(bf16[64,64,128]{2,0,1:T(8,128)(2,1)} %copy.33), calls=%async_computation.1 | async-start | bytes 2097152 | tf_op jit(solution)/shard_map/all_to_all | solution.py:65
  62.4 44.6 %all-gather.2.cloned.1.call-done = bf16[64,3,4096]{2,0,1:T(8,128)(2,1)} async-done(((bf16[8,3,4096]{2,0,1:T(8,128)(2,1)}), bf16[64,3,4096]{2,0,1:T(8,128)(2,1)}) %all-gather.2.cloned.1.call-update) | async-done | bytes 1572880 | tf_op jit(solution)/shard_map/all_gather | solution.py:19
  107.0 4.1 %copy.32 = bf16[8,8,3,4096]{3,2,1,0:T(4,128)(2,1)} copy(bf16[8,8,3,4096]{3,0,1,2:T(8,128)(2,1)} %bitcast.41) | data formatting | bytes 3145728 | tf_op jit(solution)/shard_map/transpose | solution.py:23
  111.1 3.1 %reshape_reshape.3 = bf16[192,4096]{1,0:T(8,128)(2,1)S(1)} reshape(bf16[8,8,3,4096]{3,2,1,0:T(4,128)(2,1)} %copy.32) | data formatting | bytes 3145728 | tf_op jit(solution)/shard_map/reshape;reshape | solution.py:13
  114.2 1.8 fusion.4
  116.0 0.0 all-to-all-done.1
  116.0 0.0 copy-done
  116.1 3.4 %convolution_convert_fusion = bf16[192,4096]{1,0:T(8,128)(2,1)} fusion(bf16[4096,128]{1,0:T(8,128)(2,1)} %bitcast.12, bf16[192,4096]{1,0:T(8,128)(2,1)S(1)} %reshape_reshape.3, bf16[1,4096,128]{2,1,0:T(8,128)(2,1)S(1)} %copy-done, f32[192,128]{1,0:T(8,128)S(1)} %fusion.4), kind=kOutput, calls=%fused_computation | convolution fusion | flops 403587072 | bytes 5341184 | tf_op jit(solution)/shard_map/dot_general | solution.py:67
  119.5 4.1 %reshape.21 = bf16[64,3,4096]{2,1,0:T(4,128)(2,1)} reshape(bf16[192,4096]{1,0:T(8,128)(2,1)} %convolution_convert_fusion) | data formatting | bytes 3145728 | tf_op jit(solution)/shard_map/reshape | solution.py:32
  123.6 0.0 copy-start.2
  123.6 9.2 %all-to-all-start.2 = ((bf16[64,3,4096]{2,1,0:T(4,128)(2,1)}), bf16[64,3,4096]{2,1,0:T(4,128)(2,1)S(1)}, u32[]{:S(2)}, u32[]{:S(2)}) async-start(bf16[64,3,4096]{2,1,0:T(4,128)(2,1)} %reshape.21), calls=%async_computation.2 | async-start | bytes 4194304 | tf_op jit(solution)/shard_map/all_to_all | solution.py:37
  132.8 0.0 copy-done.2
  132.8 0.1 copy.28
  132.9 51.9 %all-to-all-done.2 = bf16[64,3,4096]{2,1,0:T(4,128)(2,1)S(1)} async-done(((bf16[64,3,4096]{2,1,0:T(4,128)(2,1)}), bf16[64,3,4096]{2,1,0:T(4,128)(2,1)S(1)}, u32[]{:S(2)}, u32[]{:S(2)}) %all-to-all-start.2) | async-done | bytes 1572896 | tf_op jit(solution)/shard_map/all_to_all | solution.py:37
  184.8 1.5 reduce_sum.32
  186.3 3.3 %all-to-all-start.3 = ((bf16[3,8,512]{2,0,1:T(4,128)(2,1)}), bf16[3,8,512]{2,0,1:T(4,128)(2,1)S(1)}, u32[]{:S(2)}, u32[]{:S(2)}) async-start(bf16[3,8,512]{2,0,1:T(4,128)(2,1)} %bitcast.13), calls=%async_computation.3 | async-start | bytes 65536 | tf_op jit(solution)/shard_map/all_to_all | solution.py:73
  189.7 0.1 select_reduce_fusion
  189.8 5.3 %all-to-all-done.3 = bf16[3,8,512]{2,0,1:T(4,128)(2,1)S(1)} async-done(((bf16[3,8,512]{2,0,1:T(4,128)(2,1)}), bf16[3,8,512]{2,0,1:T(4,128)(2,1)S(1)}, u32[]{:S(2)}, u32[]{:S(2)}) %all-to-all-start.3) | async-done | bytes 24608 | tf_op jit(solution)/shard_map/all_to_all | solution.py:73
  195.0 0.8 fusion.1
  (4 shorter events, 0.1 us)
Async XLA Ops:
  6.5 109.5 %copy-start = (bf16[1,4096,128]{2,1,0:T(8,128)(2,1)S(1)}, bf16[1,4096,128]{2,1,0:T(8,128)(2,1)}, u32[]{:S(2)}) copy-start(bf16[1,4096,128]{2,1,0:T(8,128)(2,1)} %param.10) | copy-start | bytes 3145732
  6.5 37.4 %copy-start.1 = (bf16[1,64,8192]{2,1,0:T(8,128)(2,1)S(1)}, bf16[1,64,8192]{2,1,0:T(8,128)(2,1)}, u32[]{:S(2)}) copy-start(bf16[1,64,8192]{2,1,0:T(8,128)(2,1)} %param.11) | copy-start | bytes 3145732
  6.5 100.4 %all-gather.2.cloned.1.call-start = ((), (), s32[]{:S(2)}) async-start(), calls=%async_computation.4 | async-start | bytes 1769472 | tf_op jit(solution)/shard_map/all_gather | solution.py:19
  45.9 70.1 %all-to-all-start.1 = ((bf16[64,64,128]{2,0,1:T(8,128)(2,1)}), bf16[64,64,128]{2,0,1:T(8,128)(2,1)}, u32[]{:S(2)}, u32[]{:S(2)}) async-start(bf16[64,64,128]{2,0,1:T(8,128)(2,1)} %copy.33), calls=%async_computation.1 | async-start | bytes 2097152 | tf_op jit(solution)/shard_map/all_to_all | solution.py:65
  123.6 9.2 %copy-start.2 = (f32[6,2]{0,1:T(2,128)S(1)}, f32[6,2]{0,1:T(2,128)}, u32[]{:S(2)}) copy-start(f32[6,2]{0,1:T(2,128)} %param.8) | copy-start | bytes 148
  123.6 61.3 %all-to-all-start.2 = ((bf16[64,3,4096]{2,1,0:T(4,128)(2,1)}), bf16[64,3,4096]{2,1,0:T(4,128)(2,1)S(1)}, u32[]{:S(2)}, u32[]{:S(2)}) async-start(bf16[64,3,4096]{2,1,0:T(4,128)(2,1)} %reshape.21), calls=%async_computation.2 | async-start | bytes 4194304 | tf_op jit(solution)/shard_map/all_to_all | solution.py:37
  186.3 8.7 %all-to-all-start.3 = ((bf16[3,8,512]{2,0,1:T(4,128)(2,1)}), bf16[3,8,512]{2,0,1:T(4,128)(2,1)S(1)}, u32[]{:S(2)}, u32[]{:S(2)}) async-start(bf16[3,8,512]{2,0,1:T(4,128)(2,1)} %bitcast.13), calls=%async_computation.3 | async-start | bytes 65536 | tf_op jit(solution)/shard_map/all_to_all | solution.py:73
Sparse Core Ops, SparseCore 0:
  44.0 62.9 all-gather.1
where the time goes:
time: 203 us
  waiting for transfers between devices  102 us (50%)
  blocking collectives  34.6 us (17%)
  starting transfers between devices  29 us (14%)
  local copies, waits for them, and re-layouts  15.1 us (7%)
  between operations  13.5 us (7%)
  matrix products  6.91 us (3%)
    all_to_all x1, waiting for transfers between devices, sum_at_owner(): lax.all_to_all(in_blocks(value, dim, length), axis, 0, 0, tiled=True)  51.9 us
    all_gather x1, waiting for transfers between devices, all_blocks(): parts = lax.all_gather(parts, axes[k], axis=0, tiled=True)  44.6 us
    all_gather x1, blocking collectives, all_blocks(): parts = lax.all_gather(parts, axes[k], axis=0, tiled=True)  25 us
    all_to_all x1, starting transfers between devices, shards(): lax.all_to_all(down_local, SHARD, split_axis=1, concat_axis=0, tiled=True)  16.5 us
    all_to_all x1, blocking collectives, shards(): lax.all_to_all(outgoing, 'expert', split_axis=0, concat_axis=2, tiled=True)  9.54 us
    all_to_all x1, starting transfers between devices, sum_at_owner(): lax.all_to_all(in_blocks(value, dim, length), axis, 0, 0, tiled=True)  9.21 us
    all_to_all x1, waiting for transfers between devices, shards(): lax.all_to_all(expert_out, 'expert', split_axis=1, concat_axis=0, tiled=T...  5.27 us
    transpose x1, local copies, waits for them, and re-layouts, all_blocks(): parts.transpose(*turned, *range(len(turns), parts.ndim))  4.11 us
  transfers between devices with their start and end apart: 4, of which 3 were waited for; matrix products, arithmetic and copies ran while one was open for 6% of the time, Pallas kernels for 0%

commit v1 on v0

--- a/solution.py
+++ b/solution.py
@@ -16,7 +16,9 @@
 def all_blocks(value, axes, turns):
     parts = value[None]
     for k in turns:
-        parts = lax.all_gather(parts, axes[k], axis=0, tiled=True)
+        parts = jnp.concatenate(
+            lax.all_to_all(jnp.stack([parts] * lax.axis_size(axes[k])), axes[k], 0, 0), axis=0
+        )
     held = [lax.axis_size(axes[k]) for k in reversed(turns)]
     parts = parts.reshape(*held, *value.shape)
     turned = sorted(range(len(turns)), key=lambda place: turns[len(turns) - 1 - place])

time: 203 us -> 196 us (0.966)
  waiting for transfers between devices: 102 us -> 118 us
  between operations: 13.5 us -> 0.09 us
  blocking collectives: 34.6 us -> 24.9 us
    all_gather x1 -> x0, waiting for transfers between devices: 44.6 us -> none  [all_blocks(): parts = lax.all_gather(parts, axes[k], axis=0, tiled=True)]
    all_to_all x0 -> x1, waiting for transfers between devices: none -> 35.7 us  [all_blocks(): lax.all_to_all(jnp.stack([parts] * lax.axis_size(axes[k])), axes[k], 0, 0)]
    all_gather x1 -> x0, blocking collectives: 25 us -> none  [all_blocks(): parts = lax.all_gather(parts, axes[k], axis=0, tiled=True)]
    all_to_all x1, waiting for transfers between devices: 0.01 us -> 22.4 us  [shards(): lax.all_to_all(down_local, SHARD, split_axis=1, concat_axis=0, tiled=True)]
    all_to_all x0 -> x1, blocking collectives: none -> 15.4 us  [all_blocks(): lax.all_to_all(jnp.stack([parts] * lax.axis_size(axes[k])), axes[k], 0, 0)]
    all_to_all x0 -> x1, starting transfers between devices: none -> 10.3 us  [all_blocks(): lax.all_to_all(jnp.stack([parts] * lax.axis_size(axes[k])), axes[k], 0, 0)]
    all_to_all x1, starting transfers between devices: 16.5 us -> 7.84 us  [shards(): lax.all_to_all(down_local, SHARD, split_axis=1, concat_axis=0, tiled=True)]
    all_to_all x1, waiting for transfers between devices: 51.9 us -> 54.2 us  [sum_at_owner(): lax.all_to_all(in_blocks(value, dim, length), axis, 0, 0, tiled=True)]
  transfers between devices with their start and end apart: 4 -> 4, of which waited for: 3 -> 4; matrix products, arithmetic and copies ran while one was open for 6% -> 6% of each run, Pallas kernels for 0% -> 0%
where the time goes in v1:
time: 196 us
  waiting for transfers between devices  118 us (60%)
  starting transfers between devices  28.7 us (15%)
  blocking collectives  24.9 us (13%)
  local copies, waits for them, and re-layouts  15.6 us (8%)
  matrix products  6.92 us (4%)
    all_to_all x1, waiting for transfers between devices, sum_at_owner(): lax.all_to_all(in_blocks(value, dim, length), axis, 0, 0, tiled=True)  54.2 us
    all_to_all x1, waiting for transfers between devices, all_blocks(): lax.all_to_all(jnp.stack([parts] * lax.axis_size(axes[k])), axes[k], 0, 0)  35.7 us
    all_to_all x1, waiting for transfers between devices, shards(): lax.all_to_all(down_local, SHARD, split_axis=1, concat_axis=0, tiled=True)  22.4 us
    all_to_all x1, blocking collectives, all_blocks(): lax.all_to_all(jnp.stack([parts] * lax.axis_size(axes[k])), axes[k], 0, 0)  15.4 us
    all_to_all x1, starting transfers between devices, all_blocks(): lax.all_to_all(jnp.stack([parts] * lax.axis_size(axes[k])), axes[k], 0, 0)  10.3 us
    all_to_all x1, blocking collectives, shards(): lax.all_to_all(outgoing, 'expert', split_axis=0, concat_axis=2, tiled=True)  9.54 us
    all_to_all x1, starting transfers between devices, shards(): lax.all_to_all(down_local, SHARD, split_axis=1, concat_axis=0, tiled=True)  7.84 us
    all_to_all x1, starting transfers between devices, sum_at_owner(): lax.all_to_all(in_blocks(value, dim, length), axis, 0, 0, tiled=True)  7.16 us
  transfers between devices with their start and end apart: 4, of which 4 were waited for; matrix products, arithmetic and copies ran while one was open for 6% of the time, Pallas kernels for 0%

profile of v1, /device:TPU:24, one launch (start us, length us, event | category | flops | bytes accessed | tf_op | source)
XLA Modules:
  0.0 195.5 jit_solution(15443216781769864980)
XLA Ops:
  0.0 0.0 copy-start
  0.0 0.9 copy.25
  0.9 0.1 convert_reduce_fusion
  1.0 0.9 convolution_convert_fusion.1
  1.9 9.5 %all_to_all.65 = bf16[8,3,512]{2,1,0:T(4,128)(2,1)S(1)} all-to-all(bf16[8,3,512]{2,1,0:T(4,128)(2,1)S(1)} %copy.28), channel_id=1, replica_groups=mesh['expert'=8,'shard_0'=8,'shard_1'=8] {'expert'}, dimensions={0} | all-to-all | bytes 49152 | tf_op jit(solution)/shard_map/all_to_all | solution.py:58
  11.5 0.1 stack.6
  11.5 15.4 %all_to_all.66 = bf16[8,1,3,4096]{3,2,1,0:T(4,128)(2,1)S(1)} all-to-all(bf16[8,1,3,4096]{3,2,1,0:T(4,128)(2,1)S(1)} %stack.6), channel_id=1, replica_groups=mesh['expert'=8,'shard_0'=8,'shard_1'=8] {'shard_0'}, dimensions={0} | all-to-all | bytes 393216 | tf_op jit(solution)/shard_map/all_to_all | solution.py:20
  26.9 0.1 copy.29
  27.1 1.3 stack.7
  28.4 10.3 %all-to-all-start.2 = ((bf16[8,8,3,4096]{3,1,2,0:T(8,128)(2,1)}), bf16[8,8,3,4096]{3,1,2,0:T(8,128)(2,1)S(1)}, u32[]{:S(2)}, u32[]{:S(2)}) async-start(bf16[8,8,3,4096]{3,1,2,0:T(8,128)(2,1)} %stack.7), calls=%async_computation.2 | async-start | bytes 3145728 | tf_op jit(solution)/shard_map/all_to_all | solution.py:20
  38.7 1.5 copy.34
  40.2 1.7 copy.31
  41.9 35.7 %all-to-all-done.2 = bf16[8,8,3,4096]{3,1,2,0:T(8,128)(2,1)S(1)} async-done(((bf16[8,8,3,4096]{3,1,2,0:T(8,128)(2,1)}), bf16[8,8,3,4096]{3,1,2,0:T(8,128)(2,1)S(1)}, u32[]{:S(2)}, u32[]{:S(2)}) %all-to-all-start.2) | async-done | bytes 1572896 | tf_op jit(solution)/shard_map/all_to_all | solution.py:20
  77.6 7.8 %all-to-all-start.3 = ((bf16[64,64,128]{2,0,1:T(8,128)(2,1)}), bf16[64,64,128]{2,0,1:T(8,128)(2,1)}, u32[]{:S(2)}, u32[]{:S(2)}) async-start(bf16[64,64,128]{2,0,1:T(8,128)(2,1)} %copy.31), calls=%async_computation.3 | async-start | bytes 2097152 | tf_op jit(solution)/shard_map/all_to_all | solution.py:67
  85.4 2.7 %copy.30 = bf16[8,8,3,4096]{3,2,1,0:T(4,128)(2,1)} copy(bf16[8,8,3,4096]{3,0,2,1:T(8,128)(2,1)S(1)} %bitcast.39) | data formatting | bytes 3145728 | tf_op jit(solution)/shard_map/transpose | solution.py:25
  88.1 3.1 %reshape_reshape.3 = bf16[192,4096]{1,0:T(8,128)(2,1)S(1)} reshape(bf16[8,8,3,4096]{3,2,1,0:T(4,128)(2,1)} %copy.30) | data formatting | bytes 3145728 | tf_op jit(solution)/shard_map/reshape;reshape | solution.py:13
  91.3 1.8 fusion.4
  93.1 22.4 %all-to-all-done.3 = bf16[64,64,128]{2,0,1:T(8,128)(2,1)} async-done(((bf16[64,64,128]{2,0,1:T(8,128)(2,1)}), bf16[64,64,128]{2,0,1:T(8,128)(2,1)}, u32[]{:S(2)}, u32[]{:S(2)}) %all-to-all-start.3) | async-done | bytes 1048608 | tf_op jit(solution)/shard_map/all_to_all | solution.py:67
  115.5 0.0 copy-done
  115.5 3.4 %convolution_convert_fusion = bf16[192,4096]{1,0:T(8,128)(2,1)} fusion(bf16[4096,128]{1,0:T(8,128)(2,1)} %bitcast.12, bf16[192,4096]{1,0:T(8,128)(2,1)S(1)} %reshape_reshape.3, bf16[1,4096,128]{2,1,0:T(8,128)(2,1)S(1)} %copy-done, f32[192,128]{1,0:T(8,128)S(1)} %fusion.4), kind=kOutput, calls=%fused_computation | convolution fusion | flops 403587072 | bytes 5341184 | tf_op jit(solution)/shard_map/dot_general | solution.py:69
  118.9 4.1 %reshape.24 = bf16[64,3,4096]{2,1,0:T(4,128)(2,1)} reshape(bf16[192,4096]{1,0:T(8,128)(2,1)} %convolution_convert_fusion) | data formatting | bytes 3145728 | tf_op jit(solution)/shard_map/reshape | solution.py:34
  123.0 0.0 copy-start.1
  123.0 7.2 %all-to-all-start.4 = ((bf16[64,3,4096]{2,1,0:T(4,128)(2,1)}), bf16[64,3,4096]{2,1,0:T(4,128)(2,1)S(1)}, u32[]{:S(2)}, u32[]{:S(2)}) async-start(bf16[64,3,4096]{2,1,0:T(4,128)(2,1)} %reshape.24), calls=%async_computation.4 | async-start | bytes 4194304 | tf_op jit(solution)/shard_map/all_to_all | solution.py:39
  130.2 0.0 copy-done.1
  130.2 0.1 copy.26
  130.3 54.2 %all-to-all-done.4 = bf16[64,3,4096]{2,1,0:T(4,128)(2,1)S(1)} async-done(((bf16[64,3,4096]{2,1,0:T(4,128)(2,1)}), bf16[64,3,4096]{2,1,0:T(4,128)(2,1)S(1)}, u32[]{:S(2)}, u32[]{:S(2)}) %all-to-all-start.4) | async-done | bytes 1572896 | tf_op jit(solution)/shard_map/all_to_all | solution.py:39
  184.5 1.5 reduce_sum.32
  186.0 3.3 %all-to-all-start.5 = ((bf16[3,8,512]{2,0,1:T(4,128)(2,1)}), bf16[3,8,512]{2,0,1:T(4,128)(2,1)S(1)}, u32[]{:S(2)}, u32[]{:S(2)}) async-start(bf16[3,8,512]{2,0,1:T(4,128)(2,1)} %bitcast.13), calls=%async_computation.5 | async-start | bytes 65536 | tf_op jit(solution)/shard_map/all_to_all | solution.py:75
  189.3 0.1 select_reduce_fusion
  189.4 5.3 %all-to-all-done.5 = bf16[3,8,512]{2,0,1:T(4,128)(2,1)S(1)} async-done(((bf16[3,8,512]{2,0,1:T(4,128)(2,1)}), bf16[3,8,512]{2,0,1:T(4,128)(2,1)S(1)}, u32[]{:S(2)}, u32[]{:S(2)}) %all-to-all-start.5) | async-done | bytes 24608 | tf_op jit(solution)/shard_map/all_to_all | solution.py:75
  194.7 0.8 fusion.1
  (4 shorter events, 0.1 us)
Async XLA Ops:
  0.0 115.5 %copy-start = (bf16[1,4096,128]{2,1,0:T(8,128)(2,1)S(1)}, bf16[1,4096,128]{2,1,0:T(8,128)(2,1)}, u32[]{:S(2)}) copy-start(bf16[1,4096,128]{2,1,0:T(8,128)(2,1)} %param.10) | copy-start | bytes 3145732
  28.4 49.2 %all-to-all-start.2 = ((bf16[8,8,3,4096]{3,1,2,0:T(8,128)(2,1)}), bf16[8,8,3,4096]{3,1,2,0:T(8,128)(2,1)S(1)}, u32[]{:S(2)}, u32[]{:S(2)}) async-start(bf16[8,8,3,4096]{3,1,2,0:T(8,128)(2,1)} %stack.7), calls=%async_computation.2 | async-start | bytes 3145728 | tf_op jit(solution)/shard_map/all_to_all | solution.py:20
  77.6 37.9 %all-to-all-start.3 = ((bf16[64,64,128]{2,0,1:T(8,128)(2,1)}), bf16[64,64,128]{2,0,1:T(8,128)(2,1)}, u32[]{:S(2)}, u32[]{:S(2)}) async-start(bf16[64,64,128]{2,0,1:T(8,128)(2,1)} %copy.31), calls=%async_computation.3 | async-start | bytes 2097152 | tf_op jit(solution)/shard_map/all_to_all | solution.py:67
  123.0 7.2 %copy-start.1 = (f32[6,2]{0,1:T(2,128)S(1)}, f32[6,2]{0,1:T(2,128)}, u32[]{:S(2)}) copy-start(f32[6,2]{0,1:T(2,128)} %param.8) | copy-start | bytes 148
  123.0 61.5 %all-to-all-start.4 = ((bf16[64,3,4096]{2,1,0:T(4,128)(2,1)}), bf16[64,3,4096]{2,1,0:T(4,128)(2,1)S(1)}, u32[]{:S(2)}, u32[]{:S(2)}) async-start(bf16[64,3,4096]{2,1,0:T(4,128)(2,1)} %reshape.24), calls=%async_computation.4 | async-start | bytes 4194304 | tf_op jit(solution)/shard_map/all_to_all | solution.py:39
  186.0 8.7 %all-to-all-start.5 = ((bf16[3,8,512]{2,0,1:T(4,128)(2,1)}), bf16[3,8,512]{2,0,1:T(4,128)(2,1)S(1)}, u32[]{:S(2)}, u32[]{:S(2)}) async-start(bf16[3,8,512]{2,0,1:T(4,128)(2,1)} %bitcast.13), calls=%async_computation.5 | async-start | bytes 65536 | tf_op jit(solution)/shard_map/all_to_all | solution.py:75
